TPU v7x, 8 devices: a whole 2x2x1 slice. The times are simulated.
8 devices in a mesh: dp: 8 (over z, y, x, core).
Axes of the slice: x: 2, y: 2, z: 1, core: 2. Of those that a mesh axis runs over, the one named last changes fastest.
Arguments:
- u_norm: bfloat16 [16, 2048, 1536], P(None, 'dp')
- expert_idx: int32 [16, 2048, 8], P(None, 'dp')
- expert_out: bfloat16 [16, 2048, 8, 1536], P(None, 'dp')
- d_out: bfloat16 [16, 2048, 1536], P(None, 'dp')
- w_router: bfloat16 [16, 1536, 40], replicated
Outputs:
- output 1: float32 [], replicated
- output 2: float32 [16, 1536, 40], replicated
- output 3: bfloat16 [16, 2048, 1536], P(None, 'dp')
All inputs are finite; a program needn't handle non-finite values.
Results may differ from a plain program's by a relative error of at most 0.00903813.
Values sent between devices are 32-bit elements.
A program may use at most 1 GiB of HBM per device.

v0:
```python
import jax
import jax.numpy as jnp
from jax import lax
from jax.sharding import PartitionSpec as P

AUX_COEF = 0.02


def router_forward(u_norm, expert_idx, expert_out, d_out, w_router):
    num_exp = w_router.shape[2]
    one_hot = (expert_idx[..., None] == jnp.arange(num_exp)).astype(jnp.float32)
    logits = jnp.einsum('ltd,lde->lte', u_norm, w_router, preferred_element_type=jnp.float32)
    prob_vals = jax.nn.softmax(logits, axis=-1)
    chosen = jnp.sum(one_hot * logits[:, :, None, :], axis=-1)
    gate_vals = jax.nn.softmax(chosen, axis=-1)
    slot_dots = jnp.einsum('ltkd,ltd->ltk', expert_out, d_out, preferred_element_type=jnp.float32)
    return one_hot, prob_vals, gate_vals, slot_dots


def logit_grad(one_hot, prob_vals, gate_vals, slot_dots, aux_pull, loss_scale):
    d_dots = loss_scale * slot_dots
    d_chosen = gate_vals * (d_dots - jnp.sum(gate_vals * d_dots, axis=-1, keepdims=True))
    pull_row = aux_pull[:, None, :]
    aux_grad = prob_vals * (pull_row - jnp.sum(prob_vals * pull_row, axis=-1, keepdims=True))
    return jnp.sum(d_chosen[..., None] * one_hot, axis=2) + aux_grad


def solution(mesh):
    group_size = mesh.shape['dp']

    def local_step(u_norm, expert_idx, expert_out, d_out, w_router):
        num_exp = w_router.shape[2]
        top_k = expert_idx.shape[2]
        tok_all = u_norm.shape[1] * group_size
        one_hot, prob_vals, gate_vals, slot_dots = router_forward(u_norm, expert_idx, expert_out, d_out, w_router)
        local_stats = jnp.concatenate([jnp.sum(one_hot, axis=(1, 2)), jnp.sum(prob_vals, axis=1)], axis=-1)
        glob_stats = lax.psum(local_stats, 'dp')
        exp_frac = glob_stats[:, :num_exp] / (top_k * tok_all)
        prob_mean = glob_stats[:, num_exp:] / tok_all
        aux_total = AUX_COEF * num_exp * jnp.sum(exp_frac * prob_mean)
        main_part = jnp.sum(gate_vals * slot_dots)
        d_logits = logit_grad(one_hot, prob_vals, gate_vals, slot_dots, AUX_COEF * num_exp * exp_frac, float(tok_all))
        d_log16 = d_logits.astype(jnp.bfloat16)
        d_norm = jnp.einsum('lte,lde->ltd', d_log16, w_router, preferred_element_type=jnp.float32).astype(jnp.bfloat16)
        part_grad = jnp.einsum('ltd,lte->lde', u_norm, d_log16, preferred_element_type=jnp.float32)
        d_router = lax.psum(part_grad, 'dp')
        total_loss = lax.psum(main_part, 'dp') + aux_total
        return total_loss, d_router, d_norm

    tok_spec = P(None, 'dp', None)
    return jax.shard_map(local_step, mesh=mesh, in_specs=(tok_spec, tok_spec, P(None, 'dp', None, None), tok_spec, P()), out_specs=(P(), P(), tok_spec), check_vma=False)
```

profile of v0, /device:TPU:0, one launch (start us, length us, event | category | flops | bytes accessed | tf_op | source)
XLA Modules:
  0.0 195.1 jit_solution(15248599470359908759)
XLA Ops:
  7.2 0.0 copy-start
  7.2 0.0 copy-start.1
  7.2 0.0 all-reduce.3.cloned.1.call-start
  7.2 1.5 copy-done
  8.7 8.3 %fusion.31 = f32[16,256,40]{1,2,0:T(8,128)S(1)} fusion(bf16[16,256,1536]{2,1,0:T(8,128)(2,1)} %param.5, bf16[16,1536,40]{1,2,0:T(8,128)(2,1)S(1)} %copy-done), kind=kOutput, calls=%fused_computation.42 | convolution fusion | flops 503316480 | bytes 15204352 | tf_op jit(solution)/shard_map/ltd,lde->lte/dot_general | solution.py:12
  17.0 0.3 fusion.30
  17.4 0.0 copy-done.1
  17.4 1.5 select_reduce_fusion.1
  18.9 1.0 fusion.29
  19.9 54.2 %fusion.4 = f32[16,256,1,8]{3,2,1,0:T(1,128)} fusion(bf16[16,256,8,1536]{3,2,1,0:T(8,128)(2,1)} %param.7, bf16[16,256,1536,1]{2,1,0,3:T(8,128)(2,1)} %bitcast.19), kind=kOutput, calls=%fused_computation.4 | convolution fusion | flops 100663296 | bytes 113377280 | tf_op jit(solution)/shard_map/ltkd,ltd->ltk/dot_general | solution.py:16
  74.2 4.4 %copy.11 = f32[16,256,1,8]{1,3,0,2:T(8,128)S(1)} copy(f32[16,256,1,8]{3,2,1,0:T(1,128)} %fusion.4) | data formatting | bytes 262144 | tf_op jit(solution)/shard_map/ltkd,ltd->ltk/dot_general | solution.py:16
  78.5 0.7 multiply_reduce_fusion.1
  79.2 1.0 select_reduce_fusion
  80.2 0.1 pad_maximum_fusion
  80.3 25.2 %all-reduce = (f32[]{:T(128)}, f32[16,80]{1,0:T(8,128)S(1)}) all-reduce(f32[]{:T(128)} %get-tuple-element.4, f32[16,80]{1,0:T(8,128)S(1)} %pad_maximum_fusion), channel_id=1, replica_groups=mesh['dp'=8] {'dp'}, use_global_device_ids=true, to_apply=%region_4.0 | all-reduce | flops 1281 | bytes 10248 | tf_op jit(solution)/shard_map/psum | solution.py:47
  105.5 0.7 slice_multiply_fusion.1
  106.2 8.9 %convolution_bitcast_fusion = f32[16,1536,40]{1,2,0:T(8,128)} fusion(bf16[16,256,1536]{2,1,0:T(8,128)(2,1)} %param.5, f32[16,256,40]{1,2,0:T(8,128)S(1)} %get-tuple-element.5, f32[16,256,40]{1,2,0:T(8,128)S(1)} %get-tuple-element.14, f32[16,40]{1,0:T(8,128)S(1)} %get-tuple-element.9), kind=kOutput, calls=%fused_computation.11 | convolution fusion | flops 504139808 | bytes 17828352 | tf_op jit(solution)/shard_map/ltd,lte->lde/dot_general | solution.py:45
  115.1 0.0 all-reduce.3.cloned.1.call-update
  116.4 6.7 %convolution_convert_fusion = bf16[16,256,1536]{2,1,0:T(8,128)(2,1)} fusion(bf16[16,1536,40]{1,2,0:T(8,128)(2,1)S(1)} %copy-done, f32[16,256,40]{1,2,0:T(8,128)S(1)} %get-tuple-element.5, f32[16,256,40]{1,2,0:T(8,128)S(1)} %get-tuple-element.14, f32[16,40]{1,0:T(8,128)S(1)} %get-tuple-element.9), kind=kOutput, calls=%fused_computation.6 | convolution fusion | flops 510431264 | bytes 15862272 | tf_op jit(solution)/shard_map/lte,lde->ltd/dot_general | solution.py:44
  123.1 59.7 %all-reduce.3.cloned.1.call-done = f32[16,1536,40]{1,2,0:T(8,128)} async-done(((f32[16,1536,40]{1,2,0:T(8,128)}), f32[16,1536,40]{1,2,0:T(8,128)}) %all-reduce.3.cloned.1.call-update) | async-done | bytes 3932176 | tf_op jit(solution)/shard_map/psum | solution.py:46
  182.8 4.3 %copy.15 = f32[16,1536,40]{1,2,0:T(8,128)} copy(f32[16,1536,40]{1,2,0:T(8,128)} %all-reduce.3.cloned.1.call-done) | data formatting | bytes 7864320
  (1 shorter events, 0.0 us)
Async XLA Ops:
  7.2 1.6 copy-start
  7.2 10.2 %copy-start.1 = (s32[16,256,8]{1,2,0:T(8,128)S(1)}, s32[16,256,8]{1,2,0:T(8,128)}, u32[]{:S(2)}) copy-start(s32[16,256,8]{1,2,0:T(8,128)} %param.6) | copy-start | bytes 393220
  7.2 175.6 %all-reduce.3.cloned.1.call-start = ((), (), s32[]{:S(2)}) async-start(), calls=%async_computation | async-start | bytes 7864320 | tf_op jit(solution)/shard_map/psum | solution.py:46
Sparse Core Ops, SparseCore 0:
  115.2 67.5 all-reduce.2
where the time goes:
time: 196 us; the launch traced here: 195 us
  matrix products  78.2 us (40%)
  waiting for transfers between devices  59.7 us (30%)
  blocking collectives  25.2 us (13%)
  between operations  16.5 us (8%)
  local copies, waits for them, and re-layouts  10.2 us (5%)
  other arithmetic  5.34 us (3%)
    psum x1, waiting for transfers between devices, local_step(): d_router = lax.psum(part_grad, 'dp')  59.7 us
    dot_general x1, matrix products, router_forward(): jnp.einsum('ltkd,ltd->ltk', expert_out, d_out, preferred_element_type=jnp...  54.2 us
    psum x1, blocking collectives, local_step(): total_loss = lax.psum(main_part, 'dp') + aux_total  25.2 us
    dot_general x1, matrix products, local_step(): jnp.einsum('ltd,lte->lde', u_norm, d_log16, preferred_element_type=jnp.fl...  8.88 us
    dot_general x1, matrix products, router_forward(): jnp.einsum('ltd,lde->lte', u_norm, w_router, preferred_element_type=jnp.f...  8.3 us
    dot_general x1, matrix products, local_step(): jnp.einsum('lte,lde->ltd', d_log16, w_router, preferred_element_type=jnp....  6.73 us
    unnamed x5, local copies, waits for them, and re-layouts  5.82 us
    dot_general x1, local copies, waits for them, and re-layouts, router_forward(): jnp.einsum('ltkd,ltd->ltk', expert_out, d_out, preferred_element_type=jnp...  4.35 us
  transfers between devices with their start and end apart: 1, of which 1 were waited for; matrix products, arithmetic and copies ran while one was open for 3% of the time, Pallas kernels for 0%

commit v1 on v0

v1 whole, which is shorter than its diff:
```python
import functools

import jax
import jax.numpy as jnp
from jax import lax
from jax.experimental import pallas as pl
from jax.experimental.pallas import tpu as pltpu
from jax.sharding import PartitionSpec as P

AUX_COEF = 0.02
MESH = pl.DeviceIdType.MESH
RING_E = 6
RING_U = 4
RING_D = 3
LANES = 128


def stream_kernel(tok_all, idx_hbm, w_hbm, u_hbm, d_hbm, e_hbm,
                  gt_hbm, r_hbm, loss_hbm,
                  idx_v, w_v, u_v, d_v, e_v, sd_a, sd_b, cnt, rst, frac, gt_v,
                  part, rd1, rrs, rex, red, lacc, lvals,
                  in_sem, e_sem, u_sem, d_sem,
                  st_s, st_r, d1_s, d1_r, rs_s, rs_r, ex_s, ex_r, ag_s, ag_r, d2_s, d2_r,
                  ls_s, ls_r, out_sem, gt_sem):
    layers, top_k, tok = idx_v.shape
    num_exp = w_v.shape[1]
    half = tok // 2
    rows = half * top_k
    tiles = part.shape[1]
    n_dev = rst.shape[0]
    scale = float(tok_all)
    coef = AUX_COEF * num_exp

    me = lax.axis_index('dp')
    core = me % 2
    x = (me // 2) % 2
    y = me // 4
    mate = me + 1 - 2 * core
    x_peer = me + 2 - 4 * x
    y_peer = me + 4 - 8 * y
    big1 = x_peer * (1 - core) + y_peer * core
    big2 = y_peer * (1 - core) + x_peer * core
    hb = x * (1 - core) + y * core
    hs = y * (1 - core) + x * core
    base = 6 * core
    big_keep = base + 2 * hb
    big_send = base + 2 * (1 - hb)
    small_keep = base + 4 + hs
    small_send = base + 4 + (1 - hs)

    def remote(src, dst, send, recv, dev):
        return pltpu.make_async_remote_copy(src_ref=src, dst_ref=dst, send_sem=send, recv_sem=recv,
                                            device_id=(dev,), device_id_type=MESH)

    def e_copy(c):
        return pltpu.make_async_copy(e_hbm.at[c // 2, pl.ds((c % 2) * rows, rows)], e_v.at[c % RING_E], e_sem.at[c % RING_E])

    def u_copy(l):
        return pltpu.make_async_copy(u_hbm.at[l], u_v.at[l % RING_U], u_sem.at[l % RING_U])

    def d_copy(l):
        return pltpu.make_async_copy(d_hbm.at[l], d_v.at[l % RING_D], d_sem.at[l % RING_D])

    idx_copy = pltpu.make_async_copy(idx_hbm, idx_v, in_sem.at[0])
    w_copy = pltpu.make_async_copy(w_hbm, w_v, in_sem.at[1])
    idx_copy.start()
    d_copy(0).start()
    e_copy(0).start()
    e_copy(1).start()
    w_copy.start()
    u_copy(0).start()
    for l in range(1, 3):
        d_copy(l).start()
        e_copy(2 * l).start()
        e_copy(2 * l + 1).start()
        u_copy(l).start()
    u_copy(3).start()

    barrier = pltpu.get_barrier_semaphore()
    for r in range(1, n_dev):
        pl.semaphore_signal(barrier, inc=1, device_id=((me + r) % n_dev,), device_id_type=MESH)

    exp_iota = lax.broadcasted_iota(jnp.int32, (num_exp, tok), 0)
    lane_e = lax.broadcasted_iota(jnp.int32, (num_exp, LANES), 1)
    lane_8 = lax.broadcasted_iota(jnp.int32, (top_k, LANES), 1)
    idx_copy.wait()

    def count_layer(l, acc):
        ids = idx_v[l]
        hit = jnp.zeros((num_exp, tok), jnp.float32)
        for k in range(top_k):
            hit = hit + jnp.where(ids[k:k + 1, :] == exp_iota, 1.0, 0.0)
        col = jnp.sum(hit, axis=1, keepdims=True)
        return jnp.where(lane_e == l, col, acc)

    cnt[...] = lax.fori_loop(0, layers, count_layer, jnp.zeros((num_exp, LANES), jnp.float32))
    lacc[...] = jnp.zeros_like(lacc)
    w_copy.wait()
    pl.semaphore_wait(barrier, n_dev - 1)

    def stat_copy(r):
        return remote(cnt, rst.at[r], st_s.at[r], st_r.at[r], (me + r) % n_dev)

    for r in range(1, n_dev):
        stat_copy(r).start()

    def d1_copy(l):
        return remote(part.at[l, pl.ds(6 * (1 - core), 6)], rd1.at[l], d1_s.at[l], d1_r.at[l], mate)

    def rs_copies(l):
        return (remote(part.at[l, pl.ds(big_send, 2)], rrs.at[l, pl.ds(0, 2)], rs_s.at[0, l], rs_r.at[0, l], big1),
                remote(part.at[l, pl.ds(small_send, 1)], rrs.at[l, pl.ds(2, 1)], rs_s.at[1, l], rs_r.at[1, l], big2))

    def ex_copies(l):
        return (remote(part.at[l, pl.ds(big_keep, 2)], rex.at[l, pl.ds(0, 2)], ex_s.at[0, l], ex_r.at[0, l], big2),
                remote(part.at[l, pl.ds(small_keep, 1)], rex.at[l, pl.ds(2, 1)], ex_s.at[1, l], ex_r.at[1, l], big1))

    def ag_copies(l):
        return (remote(red.at[l, pl.ds(big_keep, 2)], red.at[l, pl.ds(big_keep, 2)], ag_s.at[0, l], ag_r.at[0, l], big1),
                remote(red.at[l, pl.ds(small_keep, 1)], red.at[l, pl.ds(small_keep, 1)], ag_s.at[1, l], ag_r.at[1, l], big2))

    def d2_copy(l):
        return remote(red.at[l, pl.ds(base, 6)], red.at[l, pl.ds(base, 6)], d2_s.at[l], d2_r.at[l], mate)

    def out_copy(l):
        return pltpu.make_async_copy(red.at[l], r_hbm.at[l], out_sem.at[l])

    def when_layer(l, fn):
        pl.when(jnp.logical_and(l >= 0, l < layers))(lambda: fn(l))

    def act_d1(l):
        d1_copy(l).start()

    def act_rs(l):
        d1_copy(l).wait()
        for i in range(6):
            part[l, base + i] = part[l, base + i] + rd1[l, i]
        for c in rs_copies(l):
            c.start()

    def act_ex(l):
        for c in rs_copies(l):
            c.wait()
        for i in range(2):
            part[l, big_keep + i] = part[l, big_keep + i] + rrs[l, i]
        part[l, small_keep] = part[l, small_keep] + rrs[l, 2]
        for c in ex_copies(l):
            c.start()

    def act_ag(l):
        for c in ex_copies(l):
            c.wait()
        for i in range(2):
            red[l, big_keep + i] = part[l, big_keep + i] + rex[l, i]
        red[l, small_keep] = part[l, small_keep] + rex[l, 2]
        for c in ag_copies(l):
            c.start()

    def act_d2(l):
        for c in ag_copies(l):
            c.wait()
        d2_copy(l).start()

    def act_out(l):
        d2_copy(l).wait()
        out_copy(l).start()

    def slots(s, h, sd):
        c = 2 * s + h
        dref = d_v[s % RING_D, pl.ds(h * half, half), :]
        prod = lax.dot_general(e_v[c % RING_E], dref, (((1,), (1,)), ((), ())), preferred_element_type=jnp.float32)
        accs = [jnp.zeros((top_k, LANES), jnp.float32) for _ in range(4)]
        for t in range(half):
            accs[t % 4] = jnp.where(lane_8 == t, prod[t * top_k:(t + 1) * top_k, :], accs[t % 4])
        sd[...] = (accs[0] + accs[1]) + (accs[2] + accs[3])

    def finish(l):
        u = u_v[l % RING_U]
        w = w_v[l]
        logits = lax.dot_general(w, u, (((1,), (1,)), ((), ())), preferred_element_type=jnp.float32)
        ids = idx_v[l]
        dots = jnp.concatenate([sd_a[...], sd_b[...]], axis=1) * scale
        sel = ids[0:1, :] == exp_iota
        dd = jnp.where(sel, dots[0:1, :], 0.0)
        for k in range(1, top_k):
            hit = ids[k:k + 1, :] == exp_iota
            dd = jnp.where(hit, dots[k:k + 1, :], dd)
            sel = jnp.logical_or(sel, hit)
        top = jnp.max(logits, axis=0, keepdims=True)
        ev = jnp.exp(logits - top)
        prob = ev / jnp.sum(ev, axis=0, keepdims=True)
        low = jnp.where(sel, logits, -jnp.inf)
        top_sel = jnp.max(low, axis=0, keepdims=True)
        es = jnp.where(sel, jnp.exp(jnp.minimum(logits - top_sel, 0.0)), 0.0)
        gate = es / jnp.sum(es, axis=0, keepdims=True)
        inner = jnp.sum(gate * dd, axis=0, keepdims=True)
        pull = jnp.sum(jnp.where(lane_e == l, frac[...], 0.0), axis=1, keepdims=True)
        pin = jnp.sum(prob * pull, axis=0, keepdims=True)
        grad = gate * (dd - inner) + prob * (pull - pin)
        g16 = grad.astype(jnp.bfloat16)
        gt_v[l] = g16
        lacc[...] = lacc[...] + (inner + pin)
        pg = jnp.dot(g16, u, preferred_element_type=jnp.float32)
        for t in range(tiles):
            part[l, t] = pg[:, t * LANES:(t + 1) * LANES]

    def step(s, carry):
        when_layer(s - 2, act_rs)
        when_layer(s - 3, act_ex)
        when_layer(s - 6, act_out)

        @pl.when(s == 1)
        def _():
            total = cnt[...]
            for r in range(1, n_dev):
                stat_copy(r).wait()
                total = total + rst[r]
            frac[...] = total * (coef / (top_k * tok_all))

        @pl.when(s < layers)
        def _():
            d_copy(s).wait()
            e_copy(2 * s).wait()

        @pl.when(jnp.logical_and(s >= 1, s <= layers))
        def _():
            u_copy(s - 1).wait()

        @pl.when(s == 0)
        def _():
            slots(s, 0, sd_a)

        @pl.when(jnp.logical_and(s >= 1, s < layers))
        def _():
            finish(s - 1)
            slots(s, 0, sd_a)

        @pl.when(s == layers)
        def _():
            finish(s - 1)

        @pl.when(2 * s + RING_E < 2 * layers)
        def _():
            e_copy(2 * s + RING_E).start()

        @pl.when(jnp.logical_and(s >= 1, s - 1 + RING_U < layers))
        def _():
            u_copy(s - 1 + RING_U).start()

        when_layer(s - 5, act_d2)
        when_layer(s - 4, act_ag)
        when_layer(s - 1, act_d1)

        @pl.when(s < layers)
        def _():
            e_copy(2 * s + 1).wait()
            slots(s, 1, sd_b)

        @pl.when(2 * s + 1 + RING_E < 2 * layers)
        def _():
            e_copy(2 * s + 1 + RING_E).start()

        @pl.when(s + RING_D < layers)
        def _():
            d_copy(s + RING_D).start()

        @pl.when(s == layers)
        def _():
            gt_copy.start()
            lvals[me] = jnp.broadcast_to(jnp.sum(lacc[...], axis=1, keepdims=True) * (1.0 / scale), (8, LANES))
            for r in range(1, n_dev):
                loss_copy(r).start()

        return carry

    gt_copy = pltpu.make_async_copy(gt_v, gt_hbm, gt_sem.at[0])

    def loss_copy(r):
        return remote(lvals.at[me], lvals.at[me], ls_s.at[r], ls_r.at[r], (me + r) % n_dev)

    lax.fori_loop(0, layers + 6, step, 0)

    for r in range(1, n_dev):
        loss_copy(r).wait()
    total = lvals[0]
    for r in range(1, n_dev):
        total = total + lvals[r]
    lacc[...] = jnp.concatenate([total[0:1, :], total[0:1, :]], axis=1)
    loss_out = pltpu.make_async_copy(lacc, loss_hbm, gt_sem.at[1])
    loss_out.start()
    gt_copy.wait()
    for l in range(layers):
        out_copy(l).wait()
    loss_out.wait()


def finish_kernel(gt_ref, w_ref, r_ref, loss_in, dn_ref, dr_ref, loss_ref):
    for i in range(gt_ref.shape[0]):
        dn_ref[i] = lax.dot_general(gt_ref[i], w_ref[i], (((0,), (0,)), ((), ())),
                                    preferred_element_type=jnp.float32).astype(jnp.bfloat16)
        for t in range(r_ref.shape[1]):
            dr_ref[i, :, t * LANES:(t + 1) * LANES] = r_ref[i, t]
    loss_ref[0] = loss_in[0, 0]


def solution(mesh):
    group_size = mesh.shape['dp']

    def local_step(u_norm, expert_idx, expert_out, d_out, w_router):
        layers, tok, dim = u_norm.shape
        top_k = expert_idx.shape[2]
        num_exp = w_router.shape[2]
        tiles = dim // LANES
        idx_t = jnp.transpose(expert_idx, (0, 2, 1))
        w_t = jnp.transpose(w_router, (0, 2, 1))
        e_flat = expert_out.reshape(layers, tok * top_k, dim)
        any_spec = pl.BlockSpec(memory_space=pl.ANY)
        dma = pltpu.SemaphoreType.DMA
        f32, b16 = jnp.float32, jnp.bfloat16
        gt, red, loss = pl.pallas_call(
            functools.partial(stream_kernel, tok * group_size),
            out_shape=(jax.ShapeDtypeStruct((layers, num_exp, tok), b16),
                       jax.ShapeDtypeStruct((layers, tiles, num_exp, LANES), f32),
                       jax.ShapeDtypeStruct((1, tok), f32)),
            in_specs=[any_spec] * 5,
            out_specs=(any_spec,) * 3,
            scratch_shapes=[
                pltpu.VMEM((layers, top_k, tok), jnp.int32),
                pltpu.VMEM((layers, num_exp, dim), b16),
                pltpu.VMEM((RING_U, tok, dim), b16),
                pltpu.VMEM((RING_D, tok, dim), b16),
                pltpu.VMEM((RING_E, tok * top_k // 2, dim), b16),
                pltpu.VMEM((top_k, LANES), f32),
                pltpu.VMEM((top_k, LANES), f32),
                pltpu.VMEM((num_exp, LANES), f32),
                pltpu.VMEM((group_size, num_exp, LANES), f32),
                pltpu.VMEM((num_exp, LANES), f32),
                pltpu.VMEM((layers, num_exp, tok), b16),
                pltpu.VMEM((layers, tiles, num_exp, LANES), f32),
                pltpu.VMEM((layers, tiles // 2, num_exp, LANES), f32),
                pltpu.VMEM((layers, 3, num_exp, LANES), f32),
                pltpu.VMEM((layers, 3, num_exp, LANES), f32),
                pltpu.VMEM((layers, tiles, num_exp, LANES), f32),
                pltpu.VMEM((1, tok), f32),
                pltpu.VMEM((group_size, 8, LANES), f32),
                dma((2,)), dma((RING_E,)), dma((RING_U,)), dma((RING_D,)),
                dma((group_size,)), dma((group_size,)),
                dma((layers,)), dma((layers,)),
                dma((2, layers)), dma((2, layers)),
                dma((2, layers)), dma((2, layers)),
                dma((2, layers)), dma((2, layers)),
                dma((layers,)), dma((layers,)),
                dma((group_size,)), dma((group_size,)),
                dma((layers,)), dma((2,)),
            ],
            compiler_params=pltpu.CompilerParams(collective_id=0, has_side_effects=True,
                                                 vmem_limit_bytes=56 * 1024 * 1024),
            name='router_stream',
        )(idx_t, w_t, u_norm, d_out, e_flat)
        blk = 2
        d_norm, dr_t, loss1 = pl.pallas_call(
            finish_kernel,
            grid=(layers // blk,),
            out_shape=(jax.ShapeDtypeStruct((layers, tok, dim), b16),
                       jax.ShapeDtypeStruct((layers, num_exp, dim), f32),
                       jax.ShapeDtypeStruct((1,), f32)),
            in_specs=[pl.BlockSpec((blk, num_exp, tok), lambda i: (i, 0, 0)),
                      pl.BlockSpec((blk, num_exp, dim), lambda i: (i, 0, 0)),
                      pl.BlockSpec((blk, tiles, num_exp, LANES), lambda i: (i, 0, 0, 0)),
                      pl.BlockSpec((1, tok), lambda i: (0, 0), memory_space=pltpu.SMEM)],
            out_specs=(pl.BlockSpec((blk, tok, dim), lambda i: (i, 0, 0)),
                       pl.BlockSpec((blk, num_exp, dim), lambda i: (i, 0, 0)),
                       pl.BlockSpec((1,), lambda i: (0,), memory_space=pltpu.SMEM)),
            name='router_outputs',
        )(gt, w_t, red, loss)
        return loss1.reshape(()), jnp.transpose(dr_t, (0, 2, 1)), d_norm

    tok_spec = P(None, 'dp', None)
    return jax.shard_map(local_step, mesh=mesh, in_specs=(tok_spec, tok_spec, P(None, 'dp', None, None), tok_spec, P()), out_specs=(P(), P(), tok_spec), check_vma=False)
```

time: 196 us -> 91.7 us (0.47)
  Pallas kernels: 0 us -> 90.7 us
  matrix products: 78.2 us -> 0 us
  waiting for transfers between devices: 59.7 us -> 0 us
  blocking collectives: 25.2 us -> 0 us
  between operations: 16.5 us -> 0.64 us
  local copies, waits for them, and re-layouts: 10.2 us -> 0 us
  other arithmetic: 5.34 us -> 0 us
    pallas_call x0 -> x2, Pallas kernels: none -> 90.7 us  [the longest x1 79.1 us: local_step(): pl.pallas_call(functools.partial(stream_kernel, tok * group_size), out_sh...]
    dot_general x4 -> x0, matrix products: 78.2 us -> none  [the longest x1 54.2 us: router_forward(): jnp.einsum('ltkd,ltd->ltk', expert_out, d_out, preferred_element_type=jnp...]
    psum x1 -> x0, waiting for transfers between devices: 59.7 us -> none  [local_step(): d_router = lax.psum(part_grad, 'dp')]
    psum x1 -> x0, blocking collectives: 25.2 us -> none  [local_step(): total_loss = lax.psum(main_part, 'dp') + aux_total]
    unnamed x5 -> x0, local copies, waits for them, and re-layouts: 5.82 us -> none
    dot_general x1 -> x0, local copies, waits for them, and re-layouts: 4.35 us -> none  [router_forward(): jnp.einsum('ltkd,ltd->ltk', expert_out, d_out, preferred_element_type=jnp...]
    reduce_sum x3 -> x0, other arithmetic: 3.21 us -> none  [the longest x1 1.53 us: router_forward(): chosen = jnp.sum(one_hot * logits[:, :, None, :], axis=-1)]
  transfers between devices with their start and end apart: 1 -> 0, of which waited for: 1 -> 0; matrix products, arithmetic and copies ran while one was open for 3% -> 0% of each run, Pallas kernels for 0% -> 0%
where the time goes in v1:
time: 91.7 us; the launch traced here: 91.3 us
  Pallas kernels  90.7 us (99%)
    pallas_call x1, Pallas kernels, local_step(): pl.pallas_call(functools.partial(stream_kernel, tok * group_size), out_sh...  79.1 us
    pallas_call x1, Pallas kernels, local_step(): pl.pallas_call(finish_kernel, grid=(layers // blk,), out_shape=(jax.Shape...  11.6 us

profile of v1, /device:TPU:0, one launch (start us, length us, event | category | flops | bytes accessed | tf_op | source)
XLA Modules:
  0.0 91.3 jit_solution(13651914935077164868)
XLA Ops:
  0.6 79.1 %router_stream.1 = (bf16[16,40,256]{2,1,0:T(8,128)(2,1)}, f32[16,12,40,128]{3,2,1,0:T(8,128)}, f32[1,256]{1,0:T(1,128)}) custom-call(s32[16,8,256]{2,1,0:T(8,128)} %bitcast.7, bf16[16,40,1536]{2,1,0:T(8,128)(2,1)} %bitcast.5, bf16[16,256,1536]{2,1,0:T(8,128)(2,1)} %u_hbm.1, bf16[16,256,1536]{2,1,0:T(8,128)(2,1)} %d_hbm.1, bf16[16,2048,1536]{2,1,0:T(8,128)(2,1)} %bitcast.2.e_hbm), custom_call_target="tpu_custom_call" | custom-call | tf_op jit(solution)/shard_map/router_stream/pallas_call | solution.py:320
  79.8 11.6 %router_outputs.1 = (bf16[16,256,1536]{2,1,0:T(8,128)(2,1)}, f32[16,40,1536]{2,1,0:T(8,128)}, f32[1]{0:T(128)}) custom-call(bf16[16,40,256]{2,1,0:T(8,128)(2,1)} %get-tuple-element.9.gt_ref, bf16[16,40,1536]{2,1,0:T(8,128)(2,1)} %bitcast.6, f32[16,12,40,128]{3,2,1,0:T(8,128)} %get-tuple-element.10.r_ref, f32[1,256]{1,0:T(1,128)} %get-tuple-element.11.loss_in), custom_call_target="tpu_custom_call" | custom-call | tf_op jit(solution)/shard_map/router_outputs/pallas_call | solution.py:361

commit v2 on v1

v2 whole, which is shorter than its diff:
```python
import functools

import jax
import jax.numpy as jnp
from jax import lax
from jax.experimental import pallas as pl
from jax.experimental.pallas import tpu as pltpu
from jax.sharding import PartitionSpec as P

AUX_COEF = 0.02
MESH = pl.DeviceIdType.MESH
RING_E = 6
RING_U = 4
RING_D = 3
RING_P = 8
LANES = 128
OFFS = (3, 5, 9, 13, 17, 19)


def stream_kernel(tok_all, idx_hbm, w_hbm, u_hbm, d_hbm, e_hbm,
                  dn, red, loss_out,
                  idx_v, w_v, u_v, d_v, e_v, sd_a, sd_b, df_a, df_b, cnt, rst, frac, gt_v,
                  part, rd1, rrs, rex, lacc, lvals,
                  in_sem, e_sem, u_sem, d_sem,
                  st_s, st_r, d1_s, d1_r, rs_s, rs_r, ex_s, ex_r, ag_s, ag_r, d2_s, d2_r,
                  ls_s, ls_r):
    layers, top_k, tok = idx_v.shape
    num_exp = w_v.shape[1]
    half = tok // 2
    rows = half * top_k
    tiles = part.shape[1]
    n_dev = rst.shape[0]
    scale = float(tok_all)
    coef = AUX_COEF * num_exp

    me = lax.axis_index('dp')
    core = me % 2
    x = (me // 2) % 2
    y = me // 4
    mate = me + 1 - 2 * core
    x_peer = me + 2 - 4 * x
    y_peer = me + 4 - 8 * y
    big1 = x_peer * (1 - core) + y_peer * core
    big2 = y_peer * (1 - core) + x_peer * core
    hb = x * (1 - core) + y * core
    hs = y * (1 - core) + x * core
    base = 6 * core
    big_keep = base + 2 * hb
    big_send = base + 2 * (1 - hb)
    small_keep = base + 4 + hs
    small_send = base + 4 + (1 - hs)

    def remote(src, dst, send, recv, dev):
        return pltpu.make_async_remote_copy(src_ref=src, dst_ref=dst, send_sem=send, recv_sem=recv,
                                            device_id=(dev,), device_id_type=MESH)

    def e_copy(c):
        return pltpu.make_async_copy(e_hbm.at[c // 2, pl.ds((c % 2) * rows, rows)], e_v.at[c % RING_E], e_sem.at[c % RING_E])

    def u_copy(l):
        return pltpu.make_async_copy(u_hbm.at[l], u_v.at[l % RING_U], u_sem.at[l % RING_U])

    def d_copy(l):
        return pltpu.make_async_copy(d_hbm.at[l], d_v.at[l % RING_D], d_sem.at[l % RING_D])

    idx_copy = pltpu.make_async_copy(idx_hbm, idx_v, in_sem.at[0])
    w_copy = pltpu.make_async_copy(w_hbm, w_v, in_sem.at[1])
    idx_copy.start()
    d_copy(0).start()
    e_copy(0).start()
    e_copy(1).start()
    w_copy.start()
    u_copy(0).start()
    for l in range(1, 3):
        d_copy(l).start()
        e_copy(2 * l).start()
        e_copy(2 * l + 1).start()
        u_copy(l).start()
    u_copy(3).start()

    barrier = pltpu.get_barrier_semaphore()
    for r in range(1, n_dev):
        pl.semaphore_signal(barrier, inc=1, device_id=((me + r) % n_dev,), device_id_type=MESH)

    exp_iota = lax.broadcasted_iota(jnp.int32, (num_exp, tok), 0)
    lane_e = lax.broadcasted_iota(jnp.int32, (num_exp, LANES), 1)
    lane_8 = lax.broadcasted_iota(jnp.int32, (top_k, LANES), 1)
    idx_copy.wait()

    def count_layer(l, acc):
        ids = idx_v[l]
        hit = jnp.zeros((num_exp, tok), jnp.float32)
        for k in range(top_k):
            hit = hit + jnp.where(ids[k:k + 1, :] == exp_iota, 1.0, 0.0)
        col = jnp.sum(hit, axis=1, keepdims=True)
        return jnp.where(lane_e == l, col, acc)

    cnt[...] = lax.fori_loop(0, layers, count_layer, jnp.zeros((num_exp, LANES), jnp.float32))
    lacc[...] = jnp.zeros_like(lacc)
    pl.semaphore_wait(barrier, n_dev - 1)

    def stat_copy(r):
        return remote(cnt, rst.at[r], st_s.at[r], st_r.at[r], (me + r) % n_dev)

    for r in range(1, n_dev):
        stat_copy(r).start()

    def cols(l, tile, n):
        return red.at[l, :, pl.ds(pl.multiple_of(tile * LANES, LANES), n * LANES)]

    def d1_copy(l):
        return remote(part.at[l % RING_P, pl.ds(6 * (1 - core), 6)], rd1.at[l], d1_s.at[l], d1_r.at[l], mate)

    def rs_copies(l):
        return (remote(part.at[l % RING_P, pl.ds(big_send, 2)], rrs.at[l, pl.ds(0, 2)], rs_s.at[0, l], rs_r.at[0, l], big1),
                remote(part.at[l % RING_P, pl.ds(small_send, 1)], rrs.at[l, pl.ds(2, 1)], rs_s.at[1, l], rs_r.at[1, l], big2))

    def ex_copies(l):
        return (remote(part.at[l % RING_P, pl.ds(big_keep, 2)], rex.at[l, pl.ds(0, 2)], ex_s.at[0, l], ex_r.at[0, l], big2),
                remote(part.at[l % RING_P, pl.ds(small_keep, 1)], rex.at[l, pl.ds(2, 1)], ex_s.at[1, l], ex_r.at[1, l], big1))

    def ag_copies(l):
        big, small = cols(l, big_keep, 2), cols(l, small_keep, 1)
        return (remote(big, big, ag_s.at[0, l], ag_r.at[0, l], big1),
                remote(small, small, ag_s.at[1, l], ag_r.at[1, l], big2))

    def d2_copy(l):
        return remote(cols(l, base, 6), cols(l, base, 6), d2_s.at[l], d2_r.at[l], mate)

    def when_layer(l, fn):
        pl.when(jnp.logical_and(l >= 0, l < layers))(lambda: fn(l))

    def act_d1(l):
        d1_copy(l).start()

    def act_rs(l):
        d1_copy(l).wait()
        for i in range(6):
            part[l % RING_P, base + i] = part[l % RING_P, base + i] + rd1[l, i]
        for c in rs_copies(l):
            c.start()

    def act_ex(l):
        for c in rs_copies(l):
            c.wait()
        for i in range(2):
            part[l % RING_P, big_keep + i] = part[l % RING_P, big_keep + i] + rrs[l, i]
        part[l % RING_P, small_keep] = part[l % RING_P, small_keep] + rrs[l, 2]
        for c in ex_copies(l):
            c.start()

    def act_ag(l):
        for c in ex_copies(l):
            c.wait()
        for i in range(2):
            cols(l, big_keep + i, 1)[...] = part[l % RING_P, big_keep + i] + rex[l, i]
        cols(l, small_keep, 1)[...] = part[l % RING_P, small_keep] + rex[l, 2]
        for c in ag_copies(l):
            c.start()

    def act_d2(l):
        for c in ag_copies(l):
            c.wait()
        d2_copy(l).start()

    def act_out(l):
        d2_copy(l).wait()

    def slots(s, h, sd, df):
        c = 2 * s + h
        df[...] = d_v[s % RING_D, pl.ds(h * half, half), :].astype(jnp.float32)
        acc = jnp.zeros((top_k, LANES), jnp.float32)
        nm = 48
        dref = d_v[s % RING_D, pl.ds(h * half + half - nm, nm), :]
        mm = lax.dot_general(e_v[c % RING_E, (half - nm) * top_k:, :], dref, (((1,), (1,)), ((), ())), preferred_element_type=jnp.float32)
        acc2 = jnp.zeros((top_k, nm), jnp.float32)
        lane_m = lax.broadcasted_iota(jnp.int32, (top_k, nm), 1)
        for t in range(nm):
            acc2 = jnp.where(lane_m == t, mm[t * top_k:(t + 1) * top_k, :], acc2)
        for p in range((half - nm) // 2):
            ev = e_v[c % RING_E, 2 * top_k * p:2 * top_k * (p + 1), :].astype(jnp.float32)
            for i in range(2):
                t = 2 * p + i
                prod = ev[i * top_k:(i + 1) * top_k, :] * df[pl.ds(t, top_k, stride=0), :]
                lanes = prod[:, 0:LANES]
                for j in range(1, tiles):
                    lanes = lanes + prod[:, j * LANES:(j + 1) * LANES]
                acc = jnp.where(lane_8 == t, jnp.sum(lanes, axis=1, keepdims=True), acc)
        sd[...] = acc
        sd[:, half - nm:] = acc2

    def read_sd():
        return sd_a[...], sd_b[...]

    def finish(l, sd):
        u = u_v[l % RING_U]
        w = w_v[l]
        logits = lax.dot_general(w, u, (((1,), (1,)), ((), ())), preferred_element_type=jnp.float32)
        ids = idx_v[l]
        dots = jnp.concatenate(sd, axis=1) * scale
        sel = ids[0:1, :] == exp_iota
        dd = jnp.where(sel, dots[0:1, :], 0.0)
        for k in range(1, top_k):
            hit = ids[k:k + 1, :] == exp_iota
            dd = jnp.where(hit, dots[k:k + 1, :], dd)
            sel = jnp.logical_or(sel, hit)
        top = jnp.max(logits, axis=0, keepdims=True)
        ev = jnp.exp(logits - top)
        prob = ev / jnp.sum(ev, axis=0, keepdims=True)
        low = jnp.where(sel, logits, -jnp.inf)
        top_sel = jnp.max(low, axis=0, keepdims=True)
        es = jnp.where(sel, jnp.exp(jnp.minimum(logits - top_sel, 0.0)), 0.0)
        gate = es / jnp.sum(es, axis=0, keepdims=True)
        inner = jnp.sum(gate * dd, axis=0, keepdims=True)
        pull = jnp.sum(jnp.where(lane_e == l, frac[...], 0.0), axis=1, keepdims=True)
        pin = jnp.sum(prob * pull, axis=0, keepdims=True)
        grad = gate * (dd - inner) + prob * (pull - pin)
        g16 = grad.astype(jnp.bfloat16)
        gt_v[l] = g16
        lacc[...] = lacc[...] + (inner + pin)
        pg = jnp.dot(g16, u, preferred_element_type=jnp.float32)
        for t in range(tiles):
            part[l % RING_P, t] = pg[:, t * LANES:(t + 1) * LANES]

    def comm(s, h):
        for off, fn in SCHEDULE:
            if (off - h) % 2 == 0:
                when_layer(s - (off - h) // 2, fn)

    def step(s, carry):
        comm(s, 0)

        @pl.when(s == 1)
        def _():
            total = cnt[...]
            for r in range(1, n_dev):
                stat_copy(r).wait()
                total = total + rst[r]
            frac[...] = total * (coef / (top_k * tok_all))
            w_copy.wait()

        @pl.when(s < layers)
        def _():
            d_copy(s).wait()
            e_copy(2 * s).wait()

        @pl.when(jnp.logical_and(s >= 1, s <= layers))
        def _():
            u_copy(s - 1).wait()

        @pl.when(s == 0)
        def _():
            slots(s, 0, sd_a, df_a)

        @pl.when(jnp.logical_and(s >= 1, s < layers))
        def _():
            sd = read_sd()
            slots(s, 0, sd_a, df_a)
            finish(s - 1, sd)

        @pl.when(s == layers)
        def _():
            finish(s - 1, read_sd())

        @pl.when(2 * s + RING_E < 2 * layers)
        def _():
            e_copy(2 * s + RING_E).start()

        @pl.when(jnp.logical_and(s >= 1, s - 1 + RING_U < layers))
        def _():
            u_copy(s - 1 + RING_U).start()

        @pl.when(s > layers)
        def _():
            for i in range(2):
                l = jnp.minimum(2 * (s - layers - 1) + i, layers - 1)
                dn[l] = lax.dot_general(gt_v[l], w_v[l], (((0,), (0,)), ((), ())),
                                        preferred_element_type=jnp.float32).astype(jnp.bfloat16)

        comm(s, 1)

        @pl.when(s < layers)
        def _():
            e_copy(2 * s + 1).wait()
            slots(s, 1, sd_b, df_b)

        @pl.when(2 * s + 1 + RING_E < 2 * layers)
        def _():
            e_copy(2 * s + 1 + RING_E).start()

        @pl.when(s + RING_D < layers)
        def _():
            d_copy(s + RING_D).start()

        @pl.when(s == layers)
        def _():
            lvals[me] = jnp.broadcast_to(jnp.sum(lacc[...], axis=1, keepdims=True) * (1.0 / scale), (8, LANES))
            for r in range(1, n_dev):
                loss_copy(r).start()

        return carry

    SCHEDULE = ((OFFS[0], act_d1), (OFFS[1], act_rs), (OFFS[2], act_ex), (OFFS[3], act_ag), (OFFS[4], act_d2), (OFFS[5], act_out))

    def loss_copy(r):
        return remote(lvals.at[me], lvals.at[me], ls_s.at[r], ls_r.at[r], (me + r) % n_dev)

    lax.fori_loop(0, layers + OFFS[5] // 2, step, 0)

    for r in range(1, n_dev):
        loss_copy(r).wait()
    total = lvals[0]
    for r in range(1, n_dev):
        total = total + lvals[r]
    loss_out[0] = total[0, 0]


def store_kernel(dn_v, red_v, loss_in, dn_hbm, red_hbm, loss_ref, sem):
    loss_ref[0] = loss_in[0]
    copies = []
    for l in range(dn_v.shape[0]):
        copies.append(pltpu.make_async_copy(dn_v.at[l], dn_hbm.at[l], sem.at[0, l]))
        copies.append(pltpu.make_async_copy(red_v.at[l], red_hbm.at[l], sem.at[1, l]))
    for c in copies:
        c.start()
    for c in copies:
        c.wait()


def solution(mesh):
    group_size = mesh.shape['dp']

    def local_step(u_norm, expert_idx, expert_out, d_out, w_router):
        layers, tok, dim = u_norm.shape
        top_k = expert_idx.shape[2]
        num_exp = w_router.shape[2]
        tiles = dim // LANES
        idx_t = jnp.transpose(expert_idx, (0, 2, 1))
        w_t = jnp.transpose(w_router, (0, 2, 1))
        e_flat = expert_out.reshape(layers, tok * top_k, dim)
        any_spec = pl.BlockSpec(memory_space=pl.ANY)
        dma = pltpu.SemaphoreType.DMA
        f32, b16 = jnp.float32, jnp.bfloat16
        d_norm, red, loss = pl.pallas_call(
            functools.partial(stream_kernel, tok * group_size),
            out_shape=(pltpu.VMEM((layers, tok, dim), b16),
                       pltpu.VMEM((layers, num_exp, dim), f32),
                       jax.ShapeDtypeStruct((1,), f32)),
            in_specs=[any_spec] * 5,
            out_specs=(pl.BlockSpec(memory_space=pltpu.VMEM), pl.BlockSpec(memory_space=pltpu.VMEM),
                       pl.BlockSpec(memory_space=pltpu.SMEM)),
            scratch_shapes=[
                pltpu.VMEM((layers, top_k, tok), jnp.int32),
                pltpu.VMEM((layers, num_exp, dim), b16),
                pltpu.VMEM((RING_U, tok, dim), b16),
                pltpu.VMEM((RING_D, tok, dim), b16),
                pltpu.VMEM((RING_E, tok * top_k // 2, dim), b16),
                pltpu.VMEM((top_k, LANES), f32),
                pltpu.VMEM((top_k, LANES), f32),
                pltpu.VMEM((tok // 2, dim), f32),
                pltpu.VMEM((tok // 2, dim), f32),
                pltpu.VMEM((num_exp, LANES), f32),
                pltpu.VMEM((group_size, num_exp, LANES), f32),
                pltpu.VMEM((num_exp, LANES), f32),
                pltpu.VMEM((layers, num_exp, tok), b16),
                pltpu.VMEM((RING_P, tiles, num_exp, LANES), f32),
                pltpu.VMEM((layers, tiles // 2, num_exp, LANES), f32),
                pltpu.VMEM((layers, 3, num_exp, LANES), f32),
                pltpu.VMEM((layers, 3, num_exp, LANES), f32),
                pltpu.VMEM((1, tok), f32),
                pltpu.VMEM((group_size, 8, LANES), f32),
                dma((2,)), dma((RING_E,)), dma((RING_U,)), dma((RING_D,)),
                dma((group_size,)), dma((group_size,)),
                dma((layers,)), dma((layers,)),
                dma((2, layers)), dma((2, layers)),
                dma((2, layers)), dma((2, layers)),
                dma((2, layers)), dma((2, layers)),
                dma((layers,)), dma((layers,)),
                dma((group_size,)), dma((group_size,)),
            ],
            compiler_params=pltpu.CompilerParams(collective_id=0, has_side_effects=True,
                                                 vmem_limit_bytes=46 * 1024 * 1024),
            name='router_stream',
        )(idx_t, w_t, u_norm, d_out, e_flat)
        d_norm, red, loss = pl.pallas_call(
            store_kernel,
            out_shape=(jax.ShapeDtypeStruct(d_norm.shape, d_norm.dtype), jax.ShapeDtypeStruct(red.shape, red.dtype),
                       jax.ShapeDtypeStruct((1,), f32)),
            in_specs=[pl.BlockSpec(memory_space=pltpu.VMEM)] * 2 + [pl.BlockSpec(memory_space=pltpu.SMEM)],
            out_specs=(pl.BlockSpec(memory_space=pltpu.HBM),) * 2 + (pl.BlockSpec(memory_space=pltpu.SMEM),),
            scratch_shapes=[dma((2, layers))],
            compiler_params=pltpu.CompilerParams(vmem_limit_bytes=1024 * 1024),
            name='router_store',
        )(pltpu.with_memory_space_constraint(d_norm, pltpu.VMEM), pltpu.with_memory_space_constraint(red, pltpu.VMEM), loss)
        return loss.reshape(()), jnp.transpose(red, (0, 2, 1)), d_norm

    tok_spec = P(None, 'dp', None)
    return jax.shard_map(local_step, mesh=mesh, in_specs=(tok_spec, tok_spec, P(None, 'dp', None, None), tok_spec, P()), out_specs=(P(), P(), tok_spec), check_vma=False)
```

time: 91.7 us -> 69.7 us (0.76)
  Pallas kernels: 90.7 us -> 69 us
    pallas_call x1, Pallas kernels: 79.1 us -> 61.8 us  [local_step(): pl.pallas_call(functools.partial(stream_kernel, tok * group_size), out_sh...]
    pallas_call x1, Pallas kernels: 11.6 us -> 7.15 us  [local_step(): pl.pallas_call(store_kernel, out_shape=(jax.ShapeDtypeStruct(d_norm.shape...]
where the time goes in v2:
time: 69.7 us; the launch traced here: 69.6 us
  Pallas kernels  69 us (99%)
    pallas_call x1, Pallas kernels, local_step(): pl.pallas_call(functools.partial(stream_kernel, tok * group_size), out_sh...  61.8 us
    pallas_call x1, Pallas kernels, local_step(): pl.pallas_call(store_kernel, out_shape=(jax.ShapeDtypeStruct(d_norm.shape...  7.15 us

profile of v2, /device:TPU:0, one launch (start us, length us, event | category | flops | bytes accessed | tf_op | source)
XLA Modules:
  0.0 69.6 jit_solution(10020838333568314047)
XLA Ops:
  0.6 61.8 %router_stream.1 = (bf16[16,256,1536]{2,1,0:T(8,128)(2,1)S(1)}, f32[16,40,1536]{2,1,0:T(8,128)S(1)}, f32[1]{0:T(128)}) custom-call(s32[16,8,256]{2,1,0:T(8,128)} %bitcast.6, bf16[16,40,1536]{2,1,0:T(8,128)(2,1)} %bitcast.5, bf16[16,256,1536]{2,1,0:T(8,128)(2,1)} %u_hbm.1, bf16[16,256,1536]{2,1,0:T(8,128)(2,1)} %d_hbm.1, bf16[16,2048,1536]{2,1,0:T(8,128)(2,1)} %bitcast.2.e_hbm), custom_call_target="tpu_custom_call" | custom-call | tf_op jit(solution)/shard_map/router_stream/pallas_call | solution.py:344
  62.4 7.2 %router_store.1 = (bf16[16,256,1536]{2,1,0:T(8,128)(2,1)}, f32[16,40,1536]{2,1,0:T(8,128)}, f32[1]{0:T(128)}) custom-call(bf16[16,256,1536]{2,1,0:T(8,128)(2,1)S(1)} %get-tuple-element.9.dn_v, f32[16,40,1536]{2,1,0:T(8,128)S(1)} %get-tuple-element.10.red_v, f32[1]{0:T(128)} %get-tuple-element.11.loss_in), custom_call_target="tpu_custom_call" | custom-call | tf_op jit(solution)/shard_map/router_store/pallas_call | solution.py:385
